TPU v7x, 1024 devices: a whole 8x8x8 slice. The times are simulated.
1024 devices in a mesh: row: 8 (over y), col: 8 (over x_lo, core), rep: 16 (over z, x_hi).
Axes of the slice: x: 8 (x_hi: 2, x_lo: 4; x = x_hi * 4 + x_lo), y: 8, z: 8, core: 2. Of those that a mesh axis runs over, the one named last changes fastest.
Arguments:
- hidden: bfloat16 [2048, 7168], P('rep'), may hold values from -6 to 6
- train_weight: bfloat16 [7168, 16384], P(('rep', 'row'), 'col'), may hold values from -0.0625 to 0.0625
- shard_order: int32 [8, 4, 8], replicated, may hold values from 0 to 7, each once within a row
Outputs:
- served_weight: bfloat16 [7168, 16384], P(None, ('col', 'row'))
- projected: float32 [2048, 16384], P('rep', ('col', 'row'))
Inputs may be any that keep to these rules, and one draw needn't show every extreme that they name: Each shard_order[c, k] is a permutation of 0 to 7.
All inputs are finite; a program needn't handle non-finite values.
Results may differ from a plain program's by a relative error of at most 0.001.
Values may be sent and summed in bfloat16 or wider, within the bound.
A program may use at most 32 MiB of HBM per device.

v0:
```python
import jax
import jax.numpy as jnp
from jax import lax
from jax.sharding import Mesh
from jax.sharding import PartitionSpec as P

REP = ("rep_0", "rep_1")
REP_ROW = ("rep_0", "rep_1", "row")


def gathered_by_axis(shard, axes, dim):
    filled = shard
    for number in range(len(axes) - 1, -1, -1):
        filled = lax.all_gather(filled, axes[number], axis=dim, tiled=True)
    return filled


def shards(hidden, train_weight, shard_order):
    row_count = lax.axis_size("row")
    rows_tile = train_weight.shape[0]
    cols_tile = train_weight.shape[1]
    piece_cols = cols_tile // row_count
    sub_count = shard_order.shape[1]
    sub_cols = piece_cols // sub_count
    my_order = lax.dynamic_index_in_dim(shard_order, lax.axis_index("col"), 0, keepdims=False)
    source_ids = lax.broadcasted_iota(jnp.int32, (sub_count, row_count, row_count), 2)
    selector = (my_order[:, :, None] == source_ids).astype(jnp.bfloat16)
    tiled = train_weight.reshape(rows_tile, row_count, sub_count, sub_cols)
    picked = jnp.einsum("ksj,rjkc->rskc", selector, tiled, preferred_element_type=jnp.float32)
    ordered = picked.astype(jnp.bfloat16).reshape(rows_tile, cols_tile)
    column = lax.all_to_all(ordered, "row", split_axis=1, concat_axis=0, tiled=True)
    served = gathered_by_axis(column, REP, 0)
    projected = jnp.dot(hidden, served, preferred_element_type=jnp.float32)
    return (served, projected)


def solution(mesh):
    torus = Mesh(
        mesh.devices.reshape(mesh.shape["row"], mesh.shape["col"], 8, 2),
        ("row", "col", "rep_0", "rep_1"),
    )
    return jax.shard_map(
        shards,
        mesh=torus,
        in_specs=(P(REP, None), P(REP_ROW, "col"), P()),
        out_specs=(P(None, ("col", "row")), P(REP, ("col", "row"))),
        check_vma=False,
    )
```

profile of v0, /device:TPU:1, one launch (start us, length us, event | category | flops | bytes accessed | tf_op | source)
XLA Modules:
  0.0 123.9 jit_solution(8697885949811752968)
XLA Ops:
  7.2 0.0 copy-start
  7.2 0.0 all-gather.2.cloned.1.call-start
  7.2 1.5 %reshape.14 = bf16[56,8,4,64]{3,2,1,0:T(4,128)(2,1)S(1)} reshape(bf16[56,2048]{1,0:T(8,128)(2,1)} %param.4) | data formatting | bytes 458752 | tf_op jit(solution)/shard_map/reshape | solution.py:28
  8.7 0.7 dynamic-slice_bitcast_fusion
  9.4 0.3 fusion
  9.8 0.4 copy.19
  10.1 0.3 reshape.16
  10.5 16.9 %all_to_all.19 = bf16[56,8,256]{2,0,1:T(8,128)(2,1)S(1)} all-to-all(bf16[56,8,256]{2,0,1:T(8,128)(2,1)S(1)} %reshape.16), channel_id=1, replica_groups=mesh['row'=8,'col'=8,'rep_0'=8,'rep_1'=2] {'row'}, dimensions={1} | all-to-all | bytes 458752 | tf_op jit(solution)/shard_map/all_to_all | solution.py:31
  27.3 10.3 %all_gather.6 = bf16[896,256]{1,0:T(8,128)(2,1)} all-gather(bf16[448,256]{1,0:T(8,128)(2,1)S(1)} %bitcast.18), channel_id=1, replica_groups=mesh['row'=8,'col'=8,'rep_0'=8,'rep_1'=2] {'rep_1'}, dimensions={0}, use_global_device_ids=true | all-gather | bytes 688128 | tf_op jit(solution)/shard_map/all_gather | solution.py:14
  37.6 0.0 all-gather.2.cloned.1.call-update
  37.7 71.3 %all-gather.2.cloned.1.call-done = bf16[7168,256]{1,0:T(8,128)(2,1)} async-done(((bf16[896,256]{1,0:T(8,128)(2,1)}), bf16[7168,256]{1,0:T(8,128)(2,1)}) %all-gather.2.cloned.1.call-update) | async-done | bytes 3670032 | tf_op jit(solution)/shard_map/all_gather | solution.py:14
  109.0 0.0 copy-done
  109.0 3.2 %convolution_bitcast_fusion = f32[128,256]{0,1:T(8,128)S(1)} fusion(bf16[7168,256]{1,0:T(8,128)(2,1)} %all-gather.2.cloned.1.call-done, bf16[128,7168]{1,0:T(8,128)(2,1)S(1)} %copy-done), kind=kOutput, calls=%fused_computation.2 | convolution fusion | flops 469762048 | bytes 5636096 | tf_op jit(solution)/shard_map/dot_general | solution.py:33
  112.2 0.8 copy.17
  113.0 4.1 %copy.24 = bf16[7168,256]{1,0:T(8,128)(2,1)} copy(bf16[7168,256]{1,0:T(8,128)(2,1)} %all-gather.2.cloned.1.call-done) | data formatting | bytes 7340032
Async XLA Ops:
  7.2 101.8 %copy-start = (bf16[128,7168]{1,0:T(8,128)(2,1)S(1)}, bf16[128,7168]{1,0:T(8,128)(2,1)}, u32[]{:S(2)}) copy-start(bf16[128,7168]{1,0:T(8,128)(2,1)} %param.3) | copy-start | bytes 5505028
  7.2 101.8 %all-gather.2.cloned.1.call-start = ((), (), s32[]{:S(2)}) async-start(), calls=%async_computation.1 | async-start | bytes 4128768 | tf_op jit(solution)/shard_map/all_gather | solution.py:14
Sparse Core Ops, SparseCore 0:
  37.8 71.1 all-gather.1
where the time goes:
time: 124 us
  waiting for transfers between devices  71.4 us (58%)
  blocking collectives  27.2 us (22%)
  between operations  14.1 us (11%)
  local copies, waits for them, and re-layouts  7.76 us (6%)
  matrix products  3.52 us (3%)
    all_gather x1, waiting for transfers between devices, gathered_by_axis(): filled = lax.all_gather(filled, axes[number], axis=dim, tiled=True)  71.3 us
    all_to_all x1, blocking collectives, shards(): lax.all_to_all(ordered, 'row', split_axis=1, concat_axis=0, tiled=True)  16.9 us
    all_gather x1, blocking collectives, gathered_by_axis(): filled = lax.all_gather(filled, axes[number], axis=dim, tiled=True)  10.3 us
    unnamed x4, local copies, waits for them, and re-layouts  4.88 us
    dot_general x1, matrix products, shards(): projected = jnp.dot(hidden, served, preferred_element_type=jnp.float32)  3.18 us
  transfers between devices with their start and end apart: 1, of which 1 were waited for; matrix products, arithmetic and copies ran while one was open for 0% of the time, Pallas kernels for 0%

commit v1 on v0

v1 whole, which is shorter than its diff:
```python
import functools

import jax
import jax.numpy as jnp
from jax import lax
from jax.experimental import pallas as pl
from jax.experimental.pallas import tpu as pltpu
from jax.sharding import PartitionSpec as P

MESH = pl.DeviceIdType.MESH


def handoff(
    sizes, order_ref, hidden_ref, tile_ref, served_ref, projected_ref,
    hidden, tile, pieces, hidden_sem, tile_sem, spread_send, spread_recv, near_send, near_recv, far_send, far_recv,
):
    n_row, n_z, piece_rows, cols, subs = sizes
    half_rows = n_row * piece_rows
    place_rows = 2 * half_rows
    sub_cols = cols // subs
    col = lax.axis_index("col")
    row = lax.axis_index("row")
    rep = lax.axis_index("rep")
    z, half = rep // 2, rep % 2

    lanes = 2 * sub_cols
    load_hidden = pltpu.make_async_copy(hidden_ref, hidden, hidden_sem)
    load_tile = [
        pltpu.make_async_copy(tile_ref.at[:, i * lanes : (i + 1) * lanes], tile.at[i], tile_sem.at[i])
        for i in range(tile.shape[0])
    ]
    for copy in load_tile:
        copy.start()
    load_hidden.start()

    def rep_of(dz, other):
        return lax.rem(z + dz + n_z, n_z) * 2 + (1 - half if other else half)

    def row_of(d):
        return lax.rem(row + d + n_row, n_row)

    spread = [(o, d) for o in (0, 1) for d in (1, 7, 2, 6, 3, 5, 4)]
    spread.insert(7, (1, 0))
    barrier = pltpu.get_barrier_semaphore()
    for o, d in spread:
        pl.semaphore_signal(
            barrier, inc=1, device_id={"row": row_of(d), "rep": rep_of(0, o)}, device_id_type=MESH
        )
    for dz in (1, -1):
        pl.semaphore_signal(barrier, inc=1, device_id={"rep": rep_of(dz, 0)}, device_id_type=MESH)

    for copy in load_tile:
        copy.wait()
    low = lax.broadcasted_iota(jnp.int32, (piece_rows, 2 * sub_cols), 1) < sub_cols
    for s in range(n_row):
        for pair in range(subs // 2):
            first = order_ref[col, 2 * pair, s]
            second = order_ref[col, 2 * pair + 1, s]
            a = tile[first * (subs // 2) + pair]
            b = tile[second * (subs // 2) + pair]
            pieces[s, :, pair * lanes : (pair + 1) * lanes] = jnp.where(low, a, b)

    def piece_at(of_rep, of_row):
        return pl.ds(pl.multiple_of(of_rep * half_rows + of_row * piece_rows, 8), piece_rows)

    def half_at(of_rep):
        return pl.ds(pl.multiple_of(of_rep * half_rows, 8), half_rows)

    served_ref[piece_at(rep, row), :] = pieces[row]
    pl.semaphore_wait(barrier, len(spread) + 2)

    sent = []

    def send(src, at, send_sem, recv_sem, device):
        copy = pltpu.make_async_remote_copy(
            src_ref=src, dst_ref=served_ref.at[at, :], send_sem=send_sem, recv_sem=recv_sem,
            device_id=device, device_id_type=MESH,
        )
        copy.start()
        sent.append(copy)

    def arrived(at, recv_sem, send_sem):
        ref = served_ref.at[at, :]
        pltpu.make_async_remote_copy(
            src_ref=ref, dst_ref=ref, send_sem=send_sem, recv_sem=recv_sem,
            device_id={"rep": rep_of(1, 0)}, device_id_type=MESH,
        ).wait_recv()

    DIRS = ((0, 1), (1, -1))

    def near(o, d):
        at = piece_at(rep_of(0, o), row_of(-d))
        src = pieces.at[row] if (o, d) == (0, 0) else served_ref.at[at, :]
        for way, dz in DIRS:
            send(src, at, near_send.at[way, o, d], near_recv.at[way, o, d], {"rep": rep_of(dz, 0)})

    mine = piece_at(rep, row)
    near(0, 0)
    for o, d in spread:
        send(
            pieces.at[row_of(d)], mine, spread_send.at[o, d], spread_recv.at[o, d],
            {"row": row_of(d), "rep": rep_of(0, o)},
        )
    for o, d in spread:
        arrived(piece_at(rep_of(0, o), row_of(-d)), spread_recv.at[o, d], spread_send.at[o, d])
        near(o, d)

    load_hidden.wait()

    def product(dz):
        place = lax.rem(z + dz + n_z, n_z)
        at = pl.ds(pl.multiple_of(place * place_rows, 128), place_rows)
        return jnp.dot(hidden[:, at], served_ref[at, :], preferred_element_type=jnp.float32)

    projected_ref[...] = product(0)
    last = n_z // 2
    for step in range(1, last):
        for o in (0, 1):
            for way, dz in DIRS:
                at = half_at(rep_of(-dz * step, o))
                if step == 1:
                    for d in range(n_row):
                        arrived(
                            piece_at(rep_of(-dz, o), row_of(-d)), near_recv.at[way, o, d], near_send.at[way, o, d]
                        )
                else:
                    arrived(at, far_recv.at[way, step - 2, o], far_send.at[way, step - 2, o])
                if step < last - 1 or o == way:
                    send(
                        served_ref.at[at, :], at, far_send.at[way, step - 1, o], far_recv.at[way, step - 1, o],
                        {"rep": rep_of(dz, 0)},
                    )
        projected_ref[...] += product(step)
        projected_ref[...] += product(-step)
    for way, dz in DIRS:
        arrived(half_at(rep_of(-dz * last, way)), far_recv.at[way, last - 2, way], far_send.at[way, last - 2, way])
    projected_ref[...] += product(last)
    for copy in sent:
        copy.wait_send()


def solution(mesh):
    n_row, n_rep = mesh.shape["row"], mesh.shape["rep"]

    def shards(hidden, train_weight, shard_order):
        piece_rows, tile_cols = train_weight.shape
        cols = tile_cols // n_row
        subs = shard_order.shape[1]
        n_z = n_rep // 2
        depth = hidden.shape[1]
        dma = pltpu.SemaphoreType.DMA
        return pl.pallas_call(
            functools.partial(handoff, (n_row, n_z, piece_rows, cols, subs)),
            out_shape=(
                jax.ShapeDtypeStruct((depth, cols), jnp.bfloat16),
                jax.ShapeDtypeStruct((hidden.shape[0], cols), jnp.float32),
            ),
            in_specs=[
                pl.BlockSpec(memory_space=pltpu.SMEM),
                pl.BlockSpec(memory_space=pl.ANY),
                pl.BlockSpec(memory_space=pl.ANY),
            ],
            out_specs=[pl.BlockSpec(memory_space=pltpu.VMEM)] * 2,
            scratch_shapes=[
                pltpu.VMEM(hidden.shape, jnp.bfloat16),
                pltpu.VMEM((tile_cols * subs // (2 * cols), piece_rows, 2 * cols // subs), jnp.bfloat16),
                pltpu.VMEM((n_row, piece_rows, cols), jnp.bfloat16),
                dma,
                dma((tile_cols * subs // (2 * cols),)),
                dma((2, n_row)),
                dma((2, n_row)),
                dma((2, 2, n_row)),
                dma((2, 2, n_row)),
                dma((2, n_z // 2 - 1, 2)),
                dma((2, n_z // 2 - 1, 2)),
            ],
            compiler_params=pltpu.CompilerParams(collective_id=0, has_side_effects=True),
            name="handoff",
        )(shard_order, hidden, train_weight)

    return jax.shard_map(
        shards,
        mesh=mesh,
        in_specs=(P("rep", None), P(("rep", "row"), "col"), P()),
        out_specs=(P(None, ("col", "row")), P("rep", ("col", "row"))),
        check_vma=False,
    )
```

time: 124 us -> 79.4 us (0.64)
  the two profiles are of different devices: /device:TPU:1 before, /device:TPU:16 now
where the time goes in v1:
time: 79.4 us; the launch traced here: 79.2 us
  Pallas kernels  73.7 us (93%)
  local copies, waits for them, and re-layouts  4.81 us (6%)
    pallas_call x1, Pallas kernels, shards(): pl.pallas_call(functools.partial(handoff, (n_row, n_z, piece_rows, cols,...  73.7 us
    unnamed x4, local copies, waits for them, and re-layouts  4.81 us

profile of v1, /device:TPU:16, one launch (start us, length us, event | category | flops | bytes accessed | tf_op | source)
XLA Modules:
  0.0 79.2 jit_solution(7863397937356532845)
XLA Ops:
  0.6 73.7 %handoff.1 = (bf16[7168,256]{1,0:T(8,128)(2,1)}, f32[128,256]{1,0:T(8,128)}) custom-call(s32[8,4,8]{2,1,0:T(4,128)} %order_ref.1, bf16[128,7168]{1,0:T(8,128)(2,1)} %hidden_ref.1, bf16[56,2048]{1,0:T(8,128)(2,1)} %tile_ref.1), custom_call_target="tpu_custom_call" | custom-call | tf_op jit(solution)/shard_map/handoff/pallas_call | solution.py:152
  74.4 0.0 copy-start
  74.4 4.1 %copy.7 = bf16[7168,256]{1,0:T(8,128)(2,1)} copy(bf16[7168,256]{1,0:T(8,128)(2,1)} %get-tuple-element.4) | data formatting | bytes 7340032
  78.5 0.0 copy-done
  78.5 0.7 copy.8
Async XLA Ops:
  74.4 4.2 %copy-start = (f32[128,256]{1,0:T(8,128)S(1)}, f32[128,256]{1,0:T(8,128)}, u32[]{:S(2)}) copy-start(f32[128,256]{1,0:T(8,128)} %get-tuple-element.5) | copy-start | bytes 393220

commit v2 on v0

v2 whole, which is shorter than its diff:
```python
import functools

import jax
import jax.numpy as jnp
from jax import lax
from jax.experimental import pallas as pl
from jax.experimental.pallas import tpu as pltpu
from jax.sharding import PartitionSpec as P

MESH = pl.DeviceIdType.MESH
UP, DOWN = 0, 1
STEP = {UP: 1, DOWN: -1}


def handoff(
    sizes, order_hbm, hidden_hbm, tile_hbm, served, projected,
    order, hidden, tile, pieces, relayed, local_sem, tile_sem, ready,
    row_send, row_recv, out_send, out_recv, on_send, on_recv, z_send, z_recv,
):
    n, n_x, piece_rows, cols, subs = sizes
    half_rows = n * piece_rows
    place_rows = 2 * half_rows
    lanes = 2 * cols // subs
    x_los = n_x // 2
    col = lax.axis_index("col")
    row = lax.axis_index("row")
    rep = lax.axis_index("rep")
    z, half = rep // 2, rep % 2
    x = half * x_los + col // 2

    load_order = pltpu.make_async_copy(order_hbm, order, local_sem.at[0])
    load_hidden = pltpu.make_async_copy(hidden_hbm, hidden, local_sem.at[1])
    load_tile = [
        pltpu.make_async_copy(tile_hbm.at[:, i * lanes : (i + 1) * lanes], tile.at[i], tile_sem.at[i])
        for i in range(tile.shape[0])
    ]
    load_order.start()
    for copy in load_tile:
        copy.start()
    load_hidden.start()

    def row_of(d):
        return (row + d + n) % n

    def rep_of(e, other):
        return (z + e + n) % n * 2 + (half + other) % 2

    def x_device(w):
        far = (x + 2 * w + n_x) % n_x
        return {"col": far % x_los * 2 + col % 2, "rep": z * 2 + far // x_los}

    def z_device(e):
        return {"rep": rep_of(e, 0)}

    def side(d):
        return 1 - 2 * (d // (n // 2))

    barrier = pltpu.get_barrier_semaphore()

    def greet(device):
        pl.semaphore_signal(barrier, inc=1, device_id=device, device_id_type=MESH)

    for d in range(1, n):
        greet({"row": row_of(d)})
    for w in (1, -1):
        greet(x_device(w))

    @pl.when(z < n - 1)
    def _():
        greet(z_device(1))

    @pl.when(z == 0)
    def _():
        greet(z_device(-1))

    load_order.wait()
    for copy in load_tile:
        copy.wait()
    low = lax.broadcasted_iota(jnp.int32, (piece_rows, lanes), 1) < lanes // 2
    for s in range(n):
        for pair in range(subs // 2):
            a = tile[order[col, 2 * pair, s] * (subs // 2) + pair]
            b = tile[order[col, 2 * pair + 1, s] * (subs // 2) + pair]
            pieces[s, :, pair * lanes : (pair + 1) * lanes] = jnp.where(low, a, b)

    def piece_at(of_rep, of_row):
        return pl.ds(pl.multiple_of(of_rep * half_rows + of_row * piece_rows, 8), piece_rows)

    served[piece_at(rep, row), :] = pieces[row]
    pl.semaphore_wait(barrier, n + 1 + (z + n - 2) // (n - 1) + z // (n - 1))

    @pl.when(z > 0)
    def _():
        pl.semaphore_signal(ready.at[UP], inc=1, device_id=z_device(-1), device_id_type=MESH)

    @pl.when(z == n - 1)
    def _():
        pl.semaphore_signal(ready.at[DOWN], inc=1, device_id=z_device(1), device_id_type=MESH)

    def copy_of(src, dst, send_sem, recv_sem, device):
        return pltpu.make_async_remote_copy(
            src_ref=src, dst_ref=dst, send_sem=send_sem, recv_sem=recv_sem, device_id=device, device_id_type=MESH
        )

    def await_piece(recv_sem, send_sem):
        copy_of(pieces.at[0], relayed.at[0], send_sem, recv_sem, z_device(1)).wait_recv()

    def served_piece(e, other, d):
        return served.at[piece_at(rep_of(e, other), row_of(-d)), :]

    mine = served.at[piece_at(rep, row), :]

    def nth(i):
        return (i % 2 * ((i + 1) // 2) + (1 - i % 2) * (n - i // 2)) % n

    def each(body):
        lax.fori_loop(0, n, lambda i, c: (body(nth(i)), c)[1], 0)

    for i in range(1, n):
        d = nth(i)
        copy_of(pieces.at[row_of(d)], mine, row_send.at[d], row_recv.at[d], {"row": row_of(d)}).start()

    def z_copy(way, step, other, d):
        piece = served_piece(-STEP[way] * (step - 1), other, d)
        at = (way, step - 1, other, d)
        return copy_of(piece, piece, z_send.at[at], z_recv.at[at], z_device(STEP[way]))

    def own(ways, fresh):
        def go(d):
            for way in ways:
                z_copy(way, 1, 0, d).start()
            if fresh:
                piece = served_piece(0, 0, d)
                copy_of(piece, relayed.at[d], out_send.at[d], out_recv.at[d], x_device(side(d))).start()

        def body(i, c):
            d = nth(i)
            if fresh:
                await_piece(row_recv.at[d], row_send.at[d])
            go(d)
            return c

        go(0)
        lax.fori_loop(1, n, body, 0)

    def relay(d):
        await_piece(out_recv.at[d], out_send.at[d])
        w = side(d)
        origin = (x - 2 * w + n_x) % n_x // x_los
        at = piece_at(z * 2 + origin, row_of(-d))
        copy_of(relayed.at[d], served.at[at, :], on_send.at[d], on_recv.at[d], x_device(w)).start()

    def others(ways, wait):
        def body(d):
            if wait:
                await_piece(on_recv.at[d], on_send.at[d])
            for way in ways:
                z_copy(way, 1, 1, d).start()

        each(body)

    def z_await(way, step, other, d):
        await_piece(z_recv.at[way, step - 1, other, d], z_send.at[way, step - 1, other, d])

    def z_pass(way, step, other, d):
        z_await(way, step, other, d)
        z_copy(way, step + 1, other, d).start()

    def pass_on(*moves):
        def body(d):
            for move in moves:
                z_pass(*move, d)

        each(body)

    BOTH = (DOWN, UP)

    far_down = (z > 0) & (z < 5)
    far_up = (z > 2) & (z < 7)

    def pass_third(other):
        def body(d):
            @pl.when(far_down)
            def _():
                z_pass(DOWN, 3, other, d)

            @pl.when(far_up)
            def _():
                z_pass(UP, 3, other, d)

        each(body)

    @pl.when(z == 0)
    def _():
        pl.semaphore_wait(ready.at[UP], 1)
        own((UP,), True)
        each(relay)
        others((UP,), True)
        pl.semaphore_wait(ready.at[DOWN], 1)
        own((DOWN,), False)
        pass_on((DOWN, 1, 0))
        others((DOWN,), False)
        pass_on((DOWN, 1, 1))
        pass_on((DOWN, 2, 0))
        pass_on((UP, 1, 0))
        pass_on((UP, 2, 0))
        pass_on((DOWN, 2, 1))
        pass_on((UP, 1, 1))
        pass_on((UP, 2, 1))

    @pl.when(z > 0)
    def _():
        @pl.when(z == n - 1)
        def _():
            own(BOTH, True)

        @pl.when(z < n - 1)
        def _():
            own((DOWN,), True)
            pl.semaphore_wait(ready.at[UP], 1)
            own((UP,), False)

        def body(d):
            z_pass(DOWN, 1, 0, d)
            relay(d)
            z_pass(UP, 1, 0, d)

        each(body)

        @pl.when(z == 1)
        def _():
            pass_on((DOWN, 2, 0))
            others(BOTH, True)
            pass_on((DOWN, 1, 1), (UP, 1, 1))
            pass_third(0)
            pass_on((DOWN, 2, 1), (UP, 2, 0))
            pass_third(1)
            pass_on((UP, 2, 1))

        @pl.when(z > 1)
        def _():
            pass_on((DOWN, 2, 0), (UP, 2, 0))
            others(BOTH, True)
            pass_on((DOWN, 1, 1), (UP, 1, 1))
            pass_third(0)
            pass_on((DOWN, 2, 1), (UP, 2, 1))
            pass_third(1)

    load_hidden.wait()

    def product(e):
        at = pl.ds(pl.multiple_of((z + e + n) % n * place_rows, 128), place_rows)
        return jnp.dot(hidden[:, at], served[at, :], preferred_element_type=jnp.float32)

    def sent(sem):
        copy_of(pieces.at[0], relayed.at[0], sem, sem, z_device(1)).wait_send()

    def sent_before(d):
        sent(out_send.at[d])
        sent(on_send.at[d])
        for way in BOTH:
            for other in (0, 1):
                sent(z_send.at[way, 0, other, d])

    def sent_last(d):
        for way, far in ((DOWN, far_down), (UP, far_up)):
            for other in (0, 1):
                sent(z_send.at[way, 1, other, d])
                sent(z_send.at[way, 2, other, d])

                @pl.when(far)
                def _():
                    sent(z_send.at[way, 3, other, d])

    def third_here(way, far):
        @pl.when(jnp.logical_not(far))
        def _():
            for other in (0, 1):
                each(functools.partial(z_await, way, 3, other))

    projected[...] = product(0)

    def add(e, c):
        projected[...] += product(e)
        return c

    lax.fori_loop(1, 3, lambda e, c: add(n - e, add(e, c)), 0)
    lax.fori_loop(1, n, lambda d, c: (sent(row_send.at[d]), c)[1], 0)
    each(sent_before)
    third_here(DOWN, far_down)
    projected[...] += product(3)

    @pl.when(z < n // 2)
    def _():
        for other in (0, 1):
            each(functools.partial(z_await, DOWN, 4, other))

    @pl.when(z >= n // 2)
    def _():
        for other in (0, 1):
            each(functools.partial(z_await, UP, 4, other))

    projected[...] += product(4)
    third_here(UP, far_up)
    projected[...] += product(-3)
    each(sent_last)


def solution(mesh):
    n_row, n_col, n_rep = mesh.shape["row"], mesh.shape["col"], mesh.shape["rep"]

    def shards(hidden, train_weight, shard_order):
        piece_rows, tile_cols = train_weight.shape
        cols = tile_cols // n_row
        subs = shard_order.shape[1]
        depth = hidden.shape[1]
        tiles = n_row * subs // 2
        dma = pltpu.SemaphoreType.DMA
        one = dma((n_row,))
        ring = dma((2, 4, 2, n_row))
        return pl.pallas_call(
            functools.partial(handoff, (n_row, n_col, piece_rows, cols, subs)),
            out_shape=(
                jax.ShapeDtypeStruct((depth, cols), jnp.bfloat16),
                jax.ShapeDtypeStruct((hidden.shape[0], cols), jnp.float32),
            ),
            in_specs=[pl.BlockSpec(memory_space=pltpu.HBM)] * 3,
            out_specs=[pl.BlockSpec(memory_space=pltpu.VMEM)] * 2,
            scratch_shapes=[
                pltpu.SMEM(shard_order.shape, jnp.int32),
                pltpu.VMEM(hidden.shape, jnp.bfloat16),
                pltpu.VMEM((tiles, piece_rows, tile_cols // tiles), jnp.bfloat16),
                pltpu.VMEM((n_row, piece_rows, cols), jnp.bfloat16),
                pltpu.VMEM((n_row, piece_rows, cols), jnp.bfloat16),
                dma((2,)),
                dma((tiles,)),
                pltpu.SemaphoreType.REGULAR((2,)),
                one, one, one, one, one, one, ring, ring,
            ],
            compiler_params=pltpu.CompilerParams(
                collective_id=0, has_side_effects=True, vmem_limit_bytes=16 * 1024 * 1024
            ),
            name="handoff",
        )(*[pltpu.with_memory_space_constraint(a, pltpu.HBM) for a in (shard_order, hidden, train_weight)])

    return jax.shard_map(
        shards,
        mesh=mesh,
        in_specs=(P("rep", None), P(("rep", "row"), "col"), P()),
        out_specs=(P(None, ("col", "row")), P("rep", ("col", "row"))),
        check_vma=False,
    )
```

time: 124 us -> 65.9 us (0.53)
  the two profiles are of different devices: /device:TPU:1 before, /device:TPU:4 now
where the time goes in v2:
time: 65.9 us; the launch traced here: 65.7 us
  Pallas kernels  62.6 us (95%)
  local copies, waits for them, and re-layouts  2.49 us (4%)
    pallas_call x1, Pallas kernels, shards(): pl.pallas_call(functools.partial(handoff, (n_row, n_col, piece_rows, cols...  62.6 us
    unnamed x2, local copies, waits for them, and re-layouts  2.49 us

profile of v2, /device:TPU:4, one launch (start us, length us, event | category | flops | bytes accessed | tf_op | source)
XLA Modules:
  0.0 65.7 jit_solution(9975198885501303611)
XLA Ops:
  0.6 62.6 %handoff.1 = (bf16[7168,256]{1,0:T(8,128)(2,1)S(1)}, f32[128,256]{1,0:T(8,128)S(1)}) custom-call(s32[8,4,8]{2,1,0:T(4,128)} %order_hbm.1, bf16[128,7168]{1,0:T(8,128)(2,1)} %hidden_hbm.1, bf16[56,2048]{1,0:T(8,128)(2,1)} %tile_hbm.1), custom_call_target="tpu_custom_call" | custom-call | tf_op jit(solution)/shard_map/handoff/pallas_call | solution.py:321
  63.2 1.8 %copy.7 = bf16[7168,256]{1,0:T(8,128)(2,1)} copy(bf16[7168,256]{1,0:T(8,128)(2,1)S(1)} %get-tuple-element.4) | data formatting | bytes 7340032
  65.1 0.7 copy.8

commit v3 on v2

--- a/solution.py
+++ b/solution.py
@@ -15,7 +15,7 @@
 def handoff(
     sizes, order_hbm, hidden_hbm, tile_hbm, served, projected,
     order, hidden, tile, pieces, relayed, local_sem, tile_sem, ready,
-    row_send, row_recv, out_send, out_recv, on_send, on_recv, z_send, z_recv,
+    row_recv, out_recv, on_recv, z_recv, sent,
 ):
     n, n_x, piece_rows, cols, subs = sizes
     half_rows = n * piece_rows
@@ -31,7 +31,7 @@
     load_order = pltpu.make_async_copy(order_hbm, order, local_sem.at[0])
     load_hidden = pltpu.make_async_copy(hidden_hbm, hidden, local_sem.at[1])
     load_tile = [
-        pltpu.make_async_copy(tile_hbm.at[:, i * lanes : (i + 1) * lanes], tile.at[i], tile_sem.at[i])
+        pltpu.make_async_copy(tile_hbm.at[:, i * lanes : (i + 1) * lanes], tile.at[i], tile_sem)
         for i in range(tile.shape[0])
     ]
     load_order.start()
@@ -74,8 +74,7 @@
         greet(z_device(-1))
 
     load_order.wait()
-    for copy in load_tile:
-        copy.wait()
+    pltpu.make_async_copy(tile, tile, tile_sem).wait()
     low = lax.broadcasted_iota(jnp.int32, (piece_rows, lanes), 1) < lanes // 2
     for s in range(n):
         for pair in range(subs // 2):
@@ -118,12 +117,15 @@
 
     for i in range(1, n):
         d = nth(i)
-        copy_of(pieces.at[row_of(d)], mine, row_send.at[d], row_recv.at[d], {"row": row_of(d)}).start()
+        copy_of(pieces.at[row_of(d)], mine, sent.at[0], row_recv.at[d], {"row": row_of(d)}).start()
+
+    def z_sem(way, step, other, d):
+        return z_recv.at[0 if step == n // 2 else 3 * way + step, other, d]
 
     def z_copy(way, step, other, d):
         piece = served_piece(-STEP[way] * (step - 1), other, d)
-        at = (way, step - 1, other, d)
-        return copy_of(piece, piece, z_send.at[at], z_recv.at[at], z_device(STEP[way]))
+        sem = sent.at[1 + way] if step == n // 2 else sent.at[0]
+        return copy_of(piece, piece, sem, z_sem(way, step, other, d), z_device(STEP[way]))
 
     def own(ways, fresh):
         def go(d):
@@ -131,12 +133,12 @@
                 z_copy(way, 1, 0, d).start()
             if fresh:
                 piece = served_piece(0, 0, d)
-                copy_of(piece, relayed.at[d], out_send.at[d], out_recv.at[d], x_device(side(d))).start()
+                copy_of(piece, relayed.at[d], sent.at[0], out_recv.at[d], x_device(side(d))).start()
 
         def body(i, c):
             d = nth(i)
             if fresh:
-                await_piece(row_recv.at[d], row_send.at[d])
+                await_piece(row_recv.at[d], sent.at[0])
             go(d)
             return c
 
@@ -144,23 +146,23 @@
         lax.fori_loop(1, n, body, 0)
 
     def relay(d):
-        await_piece(out_recv.at[d], out_send.at[d])
+        await_piece(out_recv.at[d], sent.at[0])
         w = side(d)
         origin = (x - 2 * w + n_x) % n_x // x_los
         at = piece_at(z * 2 + origin, row_of(-d))
-        copy_of(relayed.at[d], served.at[at, :], on_send.at[d], on_recv.at[d], x_device(w)).start()
+        copy_of(relayed.at[d], served.at[at, :], sent.at[0], on_recv.at[d], x_device(w)).start()
 
     def others(ways, wait):
         def body(d):
             if wait:
-                await_piece(on_recv.at[d], on_send.at[d])
+                await_piece(on_recv.at[d], sent.at[0])
             for way in ways:
                 z_copy(way, 1, 1, d).start()
 
         each(body)
 
     def z_await(way, step, other, d):
-        await_piece(z_recv.at[way, step - 1, other, d], z_send.at[way, step - 1, other, d])
+        await_piece(z_sem(way, step, other, d), sent.at[0])
 
     def z_pass(way, step, other, d):
         z_await(way, step, other, d)
@@ -252,25 +254,18 @@
         at = pl.ds(pl.multiple_of((z + e + n) % n * place_rows, 128), place_rows)
         return jnp.dot(hidden[:, at], served[at, :], preferred_element_type=jnp.float32)
 
-    def sent(sem):
-        copy_of(pieces.at[0], relayed.at[0], sem, sem, z_device(1)).wait_send()
-
-    def sent_before(d):
-        sent(out_send.at[d])
-        sent(on_send.at[d])
-        for way in BOTH:
-            for other in (0, 1):
-                sent(z_send.at[way, 0, other, d])
-
-    def sent_last(d):
+    def sent_pieces(sem, count):
+        ref = served.at[pl.ds(0, count * piece_rows), :]
+        copy_of(ref, ref, sem, sem, z_device(1)).wait_send()
+
+    def all_sent():
+        rest = n - 0
+        sent_pieces(sent.at[0], 3 * n - 1 + 6 * (n + rest))
         for way, far in ((DOWN, far_down), (UP, far_up)):
-            for other in (0, 1):
-                sent(z_send.at[way, 1, other, d])
-                sent(z_send.at[way, 2, other, d])
-
-                @pl.when(far)
-                def _():
-                    sent(z_send.at[way, 3, other, d])
+
+            @pl.when(far)
+            def _():
+                sent_pieces(sent.at[1 + way], n + rest)
 
     def third_here(way, far):
         @pl.when(jnp.logical_not(far))
@@ -285,8 +280,6 @@
         return c
 
     lax.fori_loop(1, 3, lambda e, c: add(n - e, add(e, c)), 0)
-    lax.fori_loop(1, n, lambda d, c: (sent(row_send.at[d]), c)[1], 0)
-    each(sent_before)
     third_here(DOWN, far_down)
     projected[...] += product(3)
 
@@ -303,7 +296,7 @@
     projected[...] += product(4)
     third_here(UP, far_up)
     projected[...] += product(-3)
-    each(sent_last)
+    all_sent()
 
 
 def solution(mesh):
@@ -317,7 +310,7 @@
         tiles = n_row * subs // 2
         dma = pltpu.SemaphoreType.DMA
         one = dma((n_row,))
-        ring = dma((2, 4, 2, n_row))
+        ring = dma((7, 2, n_row))
         return pl.pallas_call(
             functools.partial(handoff, (n_row, n_col, piece_rows, cols, subs)),
             out_shape=(
@@ -333,9 +326,9 @@
                 pltpu.VMEM((n_row, piece_rows, cols), jnp.bfloat16),
                 pltpu.VMEM((n_row, piece_rows, cols), jnp.bfloat16),
                 dma((2,)),
-                dma((tiles,)),
+                dma,
                 pltpu.SemaphoreType.REGULAR((2,)),
-                one, one, one, one, one, one, ring, ring,
+                one, one, one, ring, dma((4,)),
             ],
             compiler_params=pltpu.CompilerParams(
                 collective_id=0, has_side_effects=True, vmem_limit_bytes=16 * 1024 * 1024

time: 65.9 us -> 64 us (0.971)
  Pallas kernels: 62.6 us -> 60.7 us
    pallas_call x1, Pallas kernels: 62.6 us -> 60.7 us  [shards(): pl.pallas_call(functools.partial(handoff, (n_row, n_col, piece_rows, cols...]
where the time goes in v3:
time: 64 us; the launch traced here: 63.8 us
  Pallas kernels  60.7 us (95%)
  local copies, waits for them, and re-layouts  2.49 us (4%)
  between operations  0.64 us (1%)
    pallas_call x1, Pallas kernels, shards(): pl.pallas_call(functools.partial(handoff, (n_row, n_col, piece_rows, cols...  60.7 us
    unnamed x2, local copies, waits for them, and re-layouts  2.49 us

profile of v3, /device:TPU:4, one launch (start us, length us, event | category | flops | bytes accessed | tf_op | source)
XLA Modules:
  0.0 63.8 jit_solution(2388134724257218594)
XLA Ops:
  0.6 60.7 %handoff.1 = (bf16[7168,256]{1,0:T(8,128)(2,1)S(1)}, f32[128,256]{1,0:T(8,128)S(1)}) custom-call(s32[8,4,8]{2,1,0:T(4,128)} %order_hbm.1, bf16[128,7168]{1,0:T(8,128)(2,1)} %hidden_hbm.1, bf16[56,2048]{1,0:T(8,128)(2,1)} %tile_hbm.1), custom_call_target="tpu_custom_call" | custom-call | tf_op jit(solution)/shard_map/handoff/pallas_call | solution.py:314
  61.3 1.8 %copy.7 = bf16[7168,256]{1,0:T(8,128)(2,1)} copy(bf16[7168,256]{1,0:T(8,128)(2,1)S(1)} %get-tuple-element.4) | data formatting | bytes 7340032
  63.2 0.7 %copy.8 = f32[128,256]{1,0:T(8,128)} copy(f32[128,256]{1,0:T(8,128)S(1)} %get-tuple-element.5) | data formatting | bytes 262144

commit v4 on v3

--- a/solution.py
+++ b/solution.py
@@ -299,6 +299,18 @@
     all_sent()
 
 
+def put_out(chunks, served, projected, served_out, projected_out, sem):
+    rows = served.shape[0] // chunks
+    copies = [pltpu.make_async_copy(projected, projected_out, sem.at[chunks])] + [
+        pltpu.make_async_copy(served.at[pl.ds(i * rows, rows), :], served_out.at[pl.ds(i * rows, rows), :], sem.at[i])
+        for i in range(chunks)
+    ]
+    for copy in copies:
+        copy.start()
+    for copy in copies:
+        copy.wait()
+
+
 def solution(mesh):
     n_row, n_col, n_rep = mesh.shape["row"], mesh.shape["col"], mesh.shape["rep"]
 
@@ -311,7 +323,7 @@
         dma = pltpu.SemaphoreType.DMA
         one = dma((n_row,))
         ring = dma((7, 2, n_row))
-        return pl.pallas_call(
+        served, projected = pl.pallas_call(
             functools.partial(handoff, (n_row, n_col, piece_rows, cols, subs)),
             out_shape=(
                 jax.ShapeDtypeStruct((depth, cols), jnp.bfloat16),
@@ -335,6 +347,19 @@
             ),
             name="handoff",
         )(*[pltpu.with_memory_space_constraint(a, pltpu.HBM) for a in (shard_order, hidden, train_weight)])
+        chunks = 8
+        return pl.pallas_call(
+            functools.partial(put_out, chunks),
+            out_shape=(
+                jax.ShapeDtypeStruct(served.shape, served.dtype),
+                jax.ShapeDtypeStruct(projected.shape, projected.dtype),
+            ),
+            in_specs=[pl.BlockSpec(memory_space=pltpu.VMEM)] * 2,
+            out_specs=[pl.BlockSpec(memory_space=pltpu.HBM)] * 2,
+            scratch_shapes=[dma((chunks + 1,))],
+            compiler_params=pltpu.CompilerParams(vmem_limit_bytes=16 * 1024 * 1024),
+            name="put_out",
+        )(served, projected)
 
     return jax.shard_map(
         shards,

time: 64 us -> 63.4 us (level)
  local copies, waits for them, and re-layouts: 2.49 us -> 0 us
  Pallas kernels: 60.7 us -> 62.6 us
    unnamed x2 -> x0, local copies, waits for them, and re-layouts: 2.49 us -> none
    pallas_call x0 -> x1, Pallas kernels: none -> 1.95 us  [shards(): pl.pallas_call(functools.partial(put_out, chunks), out_shape=(jax.ShapeDt...]
where the time goes in v4:
time: 63.4 us; the launch traced here: 63.3 us
  Pallas kernels  62.6 us (99%)
  between operations  0.64 us (1%)
    pallas_call x1, Pallas kernels, shards(): pl.pallas_call(functools.partial(handoff, (n_row, n_col, piece_rows, cols...  60.7 us
    pallas_call x1, Pallas kernels, shards(): pl.pallas_call(functools.partial(put_out, chunks), out_shape=(jax.ShapeDt...  1.95 us

profile of v4, /device:TPU:4, one launch (start us, length us, event | category | flops | bytes accessed | tf_op | source)
XLA Modules:
  0.0 63.3 jit_solution(16335850288854353417)
XLA Ops:
  0.6 60.7 %handoff.1 = (bf16[7168,256]{1,0:T(8,128)(2,1)S(1)}, f32[128,256]{1,0:T(8,128)S(1)}) custom-call(s32[8,4,8]{2,1,0:T(4,128)} %order_hbm.1, bf16[128,7168]{1,0:T(8,128)(2,1)} %hidden_hbm.1, bf16[56,2048]{1,0:T(8,128)(2,1)} %tile_hbm.1), custom_call_target="tpu_custom_call" | custom-call | tf_op jit(solution)/shard_map/handoff/pallas_call | solution.py:326
  61.3 1.9 %put_out.1 = (bf16[7168,256]{1,0:T(8,128)(2,1)}, f32[128,256]{1,0:T(8,128)}) custom-call(bf16[7168,256]{1,0:T(8,128)(2,1)S(1)} %get-tuple-element.4.served, f32[128,256]{1,0:T(8,128)S(1)} %get-tuple-element.5.projected), custom_call_target="tpu_custom_call" | custom-call | tf_op jit(solution)/shard_map/put_out/pallas_call | solution.py:351

commit v5 on v4

--- a/solution.py
+++ b/solution.py
@@ -15,7 +15,7 @@
 def handoff(
     sizes, order_hbm, hidden_hbm, tile_hbm, served, projected,
     order, hidden, tile, pieces, relayed, local_sem, tile_sem, ready,
-    row_recv, out_recv, on_recv, z_recv, sent,
+    row_recv, out_recv, on_recv, z_recv, fourth_recv, sent,
 ):
     n, n_x, piece_rows, cols, subs = sizes
     half_rows = n * piece_rows
@@ -120,7 +120,7 @@
         copy_of(pieces.at[row_of(d)], mine, sent.at[0], row_recv.at[d], {"row": row_of(d)}).start()
 
     def z_sem(way, step, other, d):
-        return z_recv.at[0 if step == n // 2 else 3 * way + step, other, d]
+        return fourth_recv if step == n // 2 else z_recv.at[3 * way + step - 1, other, d]
 
     def z_copy(way, step, other, d):
         piece = served_piece(-STEP[way] * (step - 1), other, d)
@@ -283,16 +283,8 @@
     third_here(DOWN, far_down)
     projected[...] += product(3)
 
-    @pl.when(z < n // 2)
-    def _():
-        for other in (0, 1):
-            each(functools.partial(z_await, DOWN, 4, other))
-
-    @pl.when(z >= n // 2)
-    def _():
-        for other in (0, 1):
-            each(functools.partial(z_await, UP, 4, other))
-
+    fourth = served.at[pl.ds(0, 2 * half_rows), :]
+    copy_of(fourth, fourth, sent.at[0], fourth_recv, z_device(1)).wait_recv()
     projected[...] += product(4)
     third_here(UP, far_up)
     projected[...] += product(-3)
@@ -322,7 +314,7 @@
         tiles = n_row * subs // 2
         dma = pltpu.SemaphoreType.DMA
         one = dma((n_row,))
-        ring = dma((7, 2, n_row))
+        ring = dma((6, 2, n_row))
         served, projected = pl.pallas_call(
             functools.partial(handoff, (n_row, n_col, piece_rows, cols, subs)),
             out_shape=(
@@ -340,7 +332,7 @@
                 dma((2,)),
                 dma,
                 pltpu.SemaphoreType.REGULAR((2,)),
-                one, one, one, ring, dma((4,)),
+                one, one, one, ring, dma, dma((3,)),
             ],
             compiler_params=pltpu.CompilerParams(
                 collective_id=0, has_side_effects=True, vmem_limit_bytes=16 * 1024 * 1024

time: 63.4 us -> 63.3 us (level)
  no operation moved by 1% of the time
where the time goes in v5:
time: 63.3 us; the launch traced here: 63.1 us
  Pallas kernels  62.5 us (99%)
  between operations  0.64 us (1%)
    pallas_call x1, Pallas kernels, shards(): pl.pallas_call(functools.partial(handoff, (n_row, n_col, piece_rows, cols...  60.6 us
    pallas_call x1, Pallas kernels, shards(): pl.pallas_call(functools.partial(put_out, chunks), out_shape=(jax.ShapeDt...  1.95 us

profile of v5, /device:TPU:4, one launch (start us, length us, event | category | flops | bytes accessed | tf_op | source)
XLA Modules:
  0.0 63.1 jit_solution(62296398449232221)
XLA Ops:
  0.6 60.6 %handoff.1 = (bf16[7168,256]{1,0:T(8,128)(2,1)S(1)}, f32[128,256]{1,0:T(8,128)S(1)}) custom-call(s32[8,4,8]{2,1,0:T(4,128)} %order_hbm.1, bf16[128,7168]{1,0:T(8,128)(2,1)} %hidden_hbm.1, bf16[56,2048]{1,0:T(8,128)(2,1)} %tile_hbm.1), custom_call_target="tpu_custom_call" | custom-call | tf_op jit(solution)/shard_map/handoff/pallas_call | solution.py:318
  61.2 1.9 %put_out.1 = (bf16[7168,256]{1,0:T(8,128)(2,1)}, f32[128,256]{1,0:T(8,128)}) custom-call(bf16[7168,256]{1,0:T(8,128)(2,1)S(1)} %get-tuple-element.4.served, f32[128,256]{1,0:T(8,128)S(1)} %get-tuple-element.5.projected), custom_call_target="tpu_custom_call" | custom-call | tf_op jit(solution)/shard_map/put_out/pallas_call | solution.py:343
